TPU v7x, 32 devices: a whole 2x2x4 slice. The times are simulated.
32 devices in a mesh: dp: 4 (over y, core), mp: 8 (over z, x).
Axes of the slice: x: 2, y: 2, z: 4, core: 2. Of those that a mesh axis runs over, the one named last changes fastest.
Arguments:
- emb_grad: float32 [65536, 7168], P('dp', 'mp'), may hold values from -600 to 600
- mtp_grad: float32 [14336, 7168], P('dp', 'mp'), may hold values from -600 to 600
- emb_groups: int32 [64], replicated, may hold values from 0 to 31
- mtp_groups: int32 [32], replicated, may hold values from 0 to 31
- max_rms: float32 [1], replicated, may hold values from 0.5 to 2
Outputs:
- emb_clipped: bfloat16 [65536, 7168], P(('dp', 'mp'))
- mtp_clipped: bfloat16 [14336, 7168], P('dp', 'mp')
- group_rms: float32 [32], replicated
All inputs are finite; a program needn't handle non-finite values.
Results may differ from a plain program's by a relative error of at most 0.005.
Values may be sent and summed in bfloat16 or wider, within the bound.
A program may use at most 192 MiB of HBM per device.

v0:
```python
import jax
import jax.numpy as jnp
from jax import lax
from jax.sharding import PartitionSpec as P

D = 7168
V = 65536
CAT = 14336
EMB_BLK = 1024
MTP_BLK = 448
GROUPS = 32


def block_squares(gradient, block_rows):
    blocks = gradient.reshape(gradient.shape[0] // block_rows, block_rows, gradient.shape[1])
    return jnp.sum(jnp.square(blocks), axis=(1, 2))


def membership(labels):
    return (labels[:, None] == jnp.arange(GROUPS, dtype=jnp.int32)[None, :]).astype(jnp.float32)


def on_device(emb_grad, mtp_grad, emb_groups, mtp_groups, max_rms):
    shard = lax.axis_index("dp")
    embed_count = emb_grad.shape[0] // EMB_BLK
    head_count = mtp_grad.shape[0] // MTP_BLK
    embed_labels = lax.dynamic_slice_in_dim(emb_groups, shard * embed_count, embed_count)
    head_labels = lax.dynamic_slice_in_dim(mtp_groups, shard * head_count, head_count)
    emb_low = lax.optimization_barrier(emb_grad.astype(jnp.bfloat16))
    arrived = lax.all_to_all(emb_low, "mp", split_axis=0, concat_axis=1, tiled=True)
    partial_value = jnp.sum(
        block_squares(emb_grad, EMB_BLK)[:, None] * membership(embed_labels), axis=0
    )
    partial_value = partial_value + jnp.sum(
        block_squares(mtp_grad, MTP_BLK)[:, None] * membership(head_labels), axis=0
    )
    group_square = lax.psum(partial_value, ("dp", "mp"))
    group_size = jnp.sum(membership(emb_groups), axis=0) * jnp.float32(EMB_BLK * D) + jnp.sum(
        membership(mtp_groups), axis=0
    ) * jnp.float32(MTP_BLK * D)
    group_rms = jnp.sqrt(group_square / jnp.maximum(group_size, 1.0))
    global_norm = jnp.sqrt(jnp.sum(group_square))
    ceiling = max_rms[0] * jnp.sqrt(jnp.float32((V + CAT) * D))
    factor = ceiling / (global_norm + 1e-06)
    head_output = (mtp_grad * factor).astype(jnp.bfloat16)
    embed_output = (lax.optimization_barrier(arrived).astype(jnp.float32) * factor).astype(
        jnp.bfloat16
    )
    return (embed_output, head_output, group_rms)


def solution(mesh):
    placed = (P("dp", "mp"), P("dp", "mp"), P(), P(), P())
    return jax.shard_map(
        on_device,
        mesh=mesh,
        in_specs=placed,
        out_specs=(P(("dp", "mp"), None), P("dp", "mp"), P()),
        check_vma=False,
    )
```

profile of v0, /device:TPU:0, one launch (start us, length us, event | category | flops | bytes accessed | tf_op | source)
XLA Modules:
  0.0 817.1 jit_solution(17026694794706699184)
XLA Ops:
  0.6 46.9 %multiply_reduce_fusion = (f32[16384]{0:T(1024)S(1)}, bf16[16384,896]{1,0:T(8,128)(2,1)}) fusion(f32[16384,896]{1,0:T(8,128)} %param.5), kind=kLoop, calls=%fused_computation.1 | loop fusion | flops 44023808 | bytes 88145920 | tf_op jit(solution)/shard_map/reduce_sum | solution.py:16
  47.5 0.0 copy-start
  47.5 0.0 copy-start.1
  47.5 7.4 all-to-all-start
  54.9 5.6 multiply_reduce_fusion.1
  60.5 0.1 reduce_sum.82
  60.6 0.1 reduce_sum.83
  60.7 0.1 reduce_sum.79
  60.8 0.0 copy-done
  60.8 0.1 dynamic_slice.6
  60.9 0.0 copy-done.1
  60.9 0.1 dynamic_slice.7
  61.0 0.1 select_reduce_fusion.1
  61.1 0.1 select_reduce_fusion
  61.2 647.7 %psum.7 = f32[32]{0:T(128)S(1)} all-reduce(f32[32]{0:T(128)S(1)} %add.19), channel_id=1, replica_groups=mesh['dp'=4,'mp'=8] {'dp','mp'}, use_global_device_ids=true, to_apply=%region_6.0 | all-reduce | flops 32 | bytes 256 | tf_op jit(solution)/shard_map/psum | solution.py:37
  709.5 0.1 convert_reduce_fusion.1
  709.6 0.1 convert_reduce_fusion
  709.7 1.1 fusion
  711.6 8.4 %multiply_convert_fusion.1 = bf16[3584,896]{1,0:T(8,128)(2,1)} fusion(f32[3584,896]{1,0:T(8,128)} %param.6, f32[]{:T(128)S(6)} %div.6), kind=kLoop, calls=%fused_computation.2 | loop fusion | flops 6422528 | bytes 19267588 | tf_op jit(solution)/shard_map/convert_element_type | solution.py:45
  720.0 0.0 all-to-all-done
  720.0 40.7 %copy.11 = bf16[8,2048,896]{1,2,0:T(8,128)(2,1)} copy(bf16[8,2048,896]{2,1,0:T(8,128)(2,1)} %all-to-all-done) | data formatting | bytes 58720256 | tf_op jit(solution)/shard_map/all_to_all | solution.py:30
  760.7 20.3 %multiply_convert_fusion = bf16[2048,7168]{0,1:T(8,128)(2,1)} fusion(bf16[2048,7168]{0,1:T(8,128)(2,1)} %bitcast.5, f32[]{:T(128)S(6)} %div.6), kind=kLoop, calls=%fused_computation | loop fusion | flops 44040192 | bytes 58720260 | tf_op jit(solution)/shard_map/convert_element_type | solution.py:46
  780.9 36.2 %copy.12 = bf16[2048,7168]{1,0:T(8,128)(2,1)} copy(bf16[2048,7168]{0,1:T(8,128)(2,1)} %multiply_convert_fusion) | data formatting | bytes 58720256
  (2 shorter events, 0.0 us)
Async XLA Ops:
  47.5 13.3 %copy-start = (s32[64]{0:T(128)S(1)}, s32[64]{0:T(128)}, u32[]{:S(2)}) copy-start(s32[64]{0:T(128)} %param.7) | copy-start | bytes 772
  47.5 13.4 %copy-start.1 = (s32[32]{0:T(128)S(1)}, s32[32]{0:T(128)}, u32[]{:S(2)}) copy-start(s32[32]{0:T(128)} %param.8) | copy-start | bytes 388
  47.5 672.5 %all-to-all-start = ((bf16[8,2048,896]{2,1,0:T(8,128)(2,1)}), bf16[8,2048,896]{2,1,0:T(8,128)(2,1)}, u32[]{:S(2)}, u32[]{:S(2)}) async-start(bf16[8,2048,896]{2,1,0:T(8,128)(2,1)} %bitcast.6), calls=%async_computation | async-start | bytes 58720256 | tf_op jit(solution)/shard_map/all_to_all | solution.py:30
where the time goes:
time: 819 us; the launch traced here: 817 us
  blocking collectives  648 us (79%)
  other arithmetic  82.8 us (10%)
  local copies, waits for them, and re-layouts  77.2 us (9%)
    psum x1, blocking collectives, on_device(): group_square = lax.psum(partial_value, ('dp', 'mp'))  648 us
    reduce_sum x4, other arithmetic, block_squares(): return jnp.sum(jnp.square(blocks), axis=(1, 2))  52.7 us
    all_to_all x1, local copies, waits for them, and re-layouts, on_device(): lax.all_to_all(emb_low, 'mp', split_axis=0, concat_axis=1, tiled=True)  40.7 us
    unnamed x5, local copies, waits for them, and re-layouts  36.2 us
    convert_element_type x1, other arithmetic, on_device(): (lax.optimization_barrier(arrived).astype(jnp.float32) * factor).astype(j...  20.3 us
  transfers between devices with their start and end apart: 1, of which 0 were waited for; matrix products, arithmetic and copies ran while one was open for 2% of the time, Pallas kernels for 0%

commit v1 on v0

--- a/solution.py
+++ b/solution.py
@@ -27,7 +27,10 @@
     embed_labels = lax.dynamic_slice_in_dim(emb_groups, shard * embed_count, embed_count)
     head_labels = lax.dynamic_slice_in_dim(mtp_groups, shard * head_count, head_count)
     emb_low = lax.optimization_barrier(emb_grad.astype(jnp.bfloat16))
-    arrived = lax.all_to_all(emb_low, "mp", split_axis=0, concat_axis=1, tiled=True)
+    arrived = jnp.concatenate(
+        lax.all_to_all(jnp.stack(jnp.split(emb_low, lax.axis_size("mp"), axis=0)), "mp", 0, 0),
+        axis=1,
+    )
     partial_value = jnp.sum(
         block_squares(emb_grad, EMB_BLK)[:, None] * membership(embed_labels), axis=0
     )

time: 819 us -> 789 us (0.963)
  local copies, waits for them, and re-layouts: 77.2 us -> 48.5 us
    all_to_all x1 -> x0, local copies, waits for them, and re-layouts: 40.7 us -> none  [on_device(): lax.all_to_all(emb_low, 'mp', split_axis=0, concat_axis=1, tiled=True)]
    reshape x0 -> x1, local copies, waits for them, and re-layouts: none -> 20.5 us  [on_device(): jnp.concatenate(lax.all_to_all(jnp.stack(jnp.split(emb_low, lax.axis_size...]
    unnamed x5 -> x13, local copies, waits for them, and re-layouts: 36.2 us -> 25.7 us
where the time goes in v1:
time: 789 us
  blocking collectives  648 us (82%)
  other arithmetic  83 us (11%)
  local copies, waits for them, and re-layouts  48.5 us (6%)
    psum x1, blocking collectives, on_device(): group_square = lax.psum(partial_value, ('dp', 'mp'))  648 us
    reduce_sum x4, other arithmetic, block_squares(): return jnp.sum(jnp.square(blocks), axis=(1, 2))  52.7 us
    unnamed x13, local copies, waits for them, and re-layouts  25.7 us
    reshape x1, local copies, waits for them, and re-layouts, on_device(): jnp.concatenate(lax.all_to_all(jnp.stack(jnp.split(emb_low, lax.axis_size...  20.5 us
    convert_element_type x1, other arithmetic, on_device(): (lax.optimization_barrier(arrived).astype(jnp.float32) * factor).astype(j...  20.4 us
  transfers between devices with their start and end apart: 1, of which 0 were waited for; matrix products, arithmetic and copies ran while one was open for 2% of the time, Pallas kernels for 0%

profile of v1, /device:TPU:0, one launch (start us, length us, event | category | flops | bytes accessed | tf_op | source)
XLA Modules:
  0.0 788.6 jit_solution(7474511711609141693)
XLA Ops:
  0.6 46.9 %multiply_reduce_fusion = (f32[16384]{0:T(1024)S(1)}, bf16[16384,896]{1,0:T(8,128)(2,1)}) fusion(f32[16384,896]{1,0:T(8,128)} %param.5), kind=kLoop, calls=%fused_computation.1 | loop fusion | flops 44023808 | bytes 88145920 | tf_op jit(solution)/shard_map/reduce_sum | solution.py:16
  47.5 0.0 copy-start
  47.5 4.3 fusion.7
  51.8 5.0 fusion.6
  56.8 5.0 fusion.5
  61.8 4.9 fusion.4
  66.7 0.0 copy-done
  66.7 2.2 fusion.3
  68.9 2.1 fusion.2
  71.0 2.2 fusion.1
  73.2 2.1 fusion
  75.3 0.0 copy-start.1
  75.3 0.0 copy-start.2
  75.3 7.4 all-to-all-start
  82.7 5.6 multiply_reduce_fusion.1
  88.3 0.1 reduce_sum.82
  88.3 0.1 reduce_sum.79
  88.5 0.1 reduce_sum.83
  88.6 0.0 copy-done.1
  88.6 0.1 dynamic_slice.6
  88.7 0.0 copy-done.2
  88.7 0.1 dynamic_slice.7
  88.7 0.1 select_reduce_fusion
  88.8 0.1 select_reduce_fusion.1
  88.9 647.7 %psum.7 = f32[32]{0:T(128)S(1)} all-reduce(f32[32]{0:T(128)S(1)} %add.19), channel_id=1, replica_groups=mesh['dp'=4,'mp'=8] {'dp','mp'}, use_global_device_ids=true, to_apply=%region_6.0 | all-reduce | flops 32 | bytes 256 | tf_op jit(solution)/shard_map/psum | solution.py:40
  736.6 0.1 convert_reduce_fusion.1
  736.7 0.1 convert_reduce_fusion
  736.8 1.1 fusion.8
  739.3 8.4 %multiply_convert_fusion.1 = bf16[3584,896]{1,0:T(8,128)(2,1)} fusion(f32[3584,896]{1,0:T(8,128)} %param.6, f32[]{:T(128)S(6)} %div.6), kind=kLoop, calls=%fused_computation.2 | loop fusion | flops 6422528 | bytes 19267588 | tf_op jit(solution)/shard_map/convert_element_type | solution.py:48
  747.7 0.0 all-to-all-done
  747.7 20.5 %copy.10 = bf16[8,256,8,896]{3,2,0,1:T(8,128)(2,1)} copy(bf16[8,256,8,896]{3,2,1,0:T(8,128)(2,1)} %bitcast.10) | data formatting | bytes 58720256 | tf_op jit(solution)/shard_map/reshape | solution.py:30
  768.2 20.4 %multiply_convert_fusion = bf16[2048,7168]{1,0:T(8,128)(2,1)} fusion(bf16[2048,7168]{1,0:T(8,128)(2,1)} %bitcast.36, f32[]{:T(128)S(6)} %div.6), kind=kLoop, calls=%fused_computation | loop fusion | flops 44040192 | bytes 58720260 | tf_op jit(solution)/shard_map/convert_element_type | solution.py:49
  (2 shorter events, 0.0 us)
Async XLA Ops:
  47.5 19.2 %copy-start = (bf16[16384,896]{1,0:T(8,128)(2,1)S(1)}, bf16[16384,896]{1,0:T(8,128)(2,1)}, u32[]{:S(2)}) copy-start(bf16[16384,896]{1,0:T(8,128)(2,1)} %get-tuple-element.4) | copy-start | bytes 88080384
  75.3 13.3 %copy-start.1 = (s32[64]{0:T(128)S(1)}, s32[64]{0:T(128)}, u32[]{:S(2)}) copy-start(s32[64]{0:T(128)} %param.7) | copy-start | bytes 772
  75.3 13.4 %copy-start.2 = (s32[32]{0:T(128)S(1)}, s32[32]{0:T(128)}, u32[]{:S(2)}) copy-start(s32[32]{0:T(128)} %param.8) | copy-start | bytes 388
  75.3 672.4 %all-to-all-start = ((bf16[8,2048,896]{2,1,0:T(8,128)(2,1)}), bf16[8,2048,896]{2,1,0:T(8,128)(2,1)}, u32[]{:S(2)}, u32[]{:S(2)}) async-start(bf16[8,2048,896]{2,1,0:T(8,128)(2,1)} %fusion), calls=%async_computation | async-start | bytes 58720256 | tf_op jit(solution)/shard_map/all_to_all | solution.py:31

commit v2 on v0

--- a/solution.py
+++ b/solution.py
@@ -34,7 +34,7 @@
     partial_value = partial_value + jnp.sum(
         block_squares(mtp_grad, MTP_BLK)[:, None] * membership(head_labels), axis=0
     )
-    group_square = lax.psum(partial_value, ("dp", "mp"))
+    group_square = jnp.sum(lax.all_gather(partial_value, ("dp", "mp")), axis=0)
     group_size = jnp.sum(membership(emb_groups), axis=0) * jnp.float32(EMB_BLK * D) + jnp.sum(
         membership(mtp_groups), axis=0
     ) * jnp.float32(MTP_BLK * D)

time: 819 us -> 819 us (level)
    psum x1 -> x0, blocking collectives: 648 us -> none  [on_device(): group_square = lax.psum(partial_value, ('dp', 'mp'))]
    unnamed x0 -> x1, blocking collectives: none -> 648 us
    unnamed x5 -> x6, local copies, waits for them, and re-layouts: 36.2 us -> 36.2 us
where the time goes in v2:
time: 819 us; the launch traced here: 817 us
  blocking collectives  648 us (79%)
  other arithmetic  83 us (10%)
  local copies, waits for them, and re-layouts  77.2 us (9%)
    unnamed x1, blocking collectives  648 us
    reduce_sum x4, other arithmetic, block_squares(): return jnp.sum(jnp.square(blocks), axis=(1, 2))  52.7 us
    all_to_all x1, local copies, waits for them, and re-layouts, on_device(): lax.all_to_all(emb_low, 'mp', split_axis=0, concat_axis=1, tiled=True)  40.7 us
    unnamed x6, local copies, waits for them, and re-layouts  36.2 us
    convert_element_type x1, other arithmetic, on_device(): (lax.optimization_barrier(arrived).astype(jnp.float32) * factor).astype(j...  20.3 us
  transfers between devices with their start and end apart: 1, of which 0 were waited for; matrix products, arithmetic and copies ran while one was open for 2% of the time, Pallas kernels for 0%

profile of v2, /device:TPU:0, one launch (start us, length us, event | category | flops | bytes accessed | tf_op | source)
XLA Modules:
  0.0 817.2 jit_solution(12320240977675056123)
XLA Ops:
  0.6 46.9 %multiply_reduce_fusion = (f32[16384]{0:T(1024)S(1)}, bf16[16384,896]{1,0:T(8,128)(2,1)}) fusion(f32[16384,896]{1,0:T(8,128)} %param.5), kind=kLoop, calls=%fused_computation.1 | loop fusion | flops 44023808 | bytes 88145920 | tf_op jit(solution)/shard_map/reduce_sum | solution.py:16
  47.5 0.0 copy-start
  47.5 0.0 copy-start.1
  47.5 7.4 all-to-all-start
  54.9 5.6 multiply_reduce_fusion.1
  60.5 0.1 reduce_sum.91
  60.6 0.1 reduce_sum.88
  60.7 0.1 reduce_sum.92
  60.8 0.0 copy-done
  60.8 0.1 dynamic_slice.6
  60.9 0.0 copy-done.1
  60.9 0.1 dynamic_slice.7
  61.0 0.1 select_reduce_fusion
  61.1 0.1 select_reduce_fusion.1
  61.2 0.1 add_dynamic-update-slice_fusion
  61.3 647.6 %all-reduce = f32[1024]{0:T(1024)S(1)} all-reduce(f32[1024]{0:T(1024)S(1)} %add_dynamic-update-slice_fusion), channel_id=2, replica_groups=mesh['dp'=4,'mp'=8] {'dp','mp'}, use_global_device_ids=true, to_apply=%add | all-reduce | flops 1024 | bytes 8192
  708.8 0.6 reduce_sum.94
  709.4 0.1 reshape.33
  710.9 0.1 convert_reduce_fusion.1
  711.0 0.1 convert_reduce_fusion
  711.1 0.5 fusion
  711.7 8.4 %multiply_convert_fusion.1 = bf16[3584,896]{1,0:T(8,128)(2,1)} fusion(f32[3584,896]{1,0:T(8,128)} %param.6, f32[]{:T(128)S(6)} %div.6), kind=kLoop, calls=%fused_computation.2 | loop fusion | flops 6422528 | bytes 19267588 | tf_op jit(solution)/shard_map/convert_element_type | solution.py:45
  720.1 0.0 all-to-all-done
  720.1 40.7 %copy.11 = bf16[8,2048,896]{1,2,0:T(8,128)(2,1)} copy(bf16[8,2048,896]{2,1,0:T(8,128)(2,1)} %all-to-all-done) | data formatting | bytes 58720256 | tf_op jit(solution)/shard_map/all_to_all | solution.py:30
  760.8 20.3 %multiply_convert_fusion = bf16[2048,7168]{0,1:T(8,128)(2,1)} fusion(bf16[2048,7168]{0,1:T(8,128)(2,1)} %bitcast.5, f32[]{:T(128)S(6)} %div.6), kind=kLoop, calls=%fused_computation | loop fusion | flops 44040192 | bytes 58720260 | tf_op jit(solution)/shard_map/convert_element_type | solution.py:46
  781.0 36.2 %copy.12 = bf16[2048,7168]{1,0:T(8,128)(2,1)} copy(bf16[2048,7168]{0,1:T(8,128)(2,1)} %multiply_convert_fusion) | data formatting | bytes 58720256
  (3 shorter events, 0.0 us)
Async XLA Ops:
  47.5 13.3 %copy-start = (s32[64]{0:T(128)S(1)}, s32[64]{0:T(128)}, u32[]{:S(2)}) copy-start(s32[64]{0:T(128)} %param.7) | copy-start | bytes 772
  47.5 13.4 %copy-start.1 = (s32[32]{0:T(128)S(1)}, s32[32]{0:T(128)}, u32[]{:S(2)}) copy-start(s32[32]{0:T(128)} %param.8) | copy-start | bytes 388
  47.5 672.6 %all-to-all-start = ((bf16[8,2048,896]{2,1,0:T(8,128)(2,1)}), bf16[8,2048,896]{2,1,0:T(8,128)(2,1)}, u32[]{:S(2)}, u32[]{:S(2)}) async-start(bf16[8,2048,896]{2,1,0:T(8,128)(2,1)} %bitcast.6), calls=%async_computation | async-start | bytes 58720256 | tf_op jit(solution)/shard_map/all_to_all | solution.py:30
